TPU v7x, 512 devices: a whole 4x4x16 slice. The times are simulated.
512 devices in a mesh: clip: 4 (over y_lo, core), seq: 128 (over y_hi, z, x).
Axes of the slice: x: 4, y: 4 (y_hi: 2, y_lo: 2; y = y_hi * 2 + y_lo), z: 16, core: 2. Of those that a mesh axis runs over, the one named last changes fastest.
Arguments:
- temporal_queries: bfloat16 [512, 128, 1152], P(('clip', 'seq')), parts along dimension 0, may hold values from -6 to 6
- temporal_keys: bfloat16 [512, 128, 1152], P(('clip', 'seq')), parts along dimension 0, may hold values from -6 to 6
- temporal_values: bfloat16 [512, 128, 1152], P(('clip', 'seq')), parts along dimension 0, may hold values from -6 to 6
- temporal_cotangent: bfloat16 [512, 128, 1152], P(('clip', 'seq')), parts along dimension 0, may hold values from -6 to 6
- cross_queries: bfloat16 [512, 128, 1152], P(('clip', 'seq')), parts along dimension 0, may hold values from -6 to 6
- cross_cotangent: bfloat16 [512, 128, 1152], P(('clip', 'seq')), parts along dimension 0, may hold values from -24 to 24
- text_keys: bfloat16 [640, 1152], P('clip'), parts along dimension 0, may hold values from -6 to 6
- text_values: bfloat16 [640, 1152], P('clip'), parts along dimension 0, may hold values from -6 to 6
- text_length: int32 [4], P('clip'), parts along dimension 0, may hold values from 80 to 160
Outputs:
- temporal_queries_grad: bfloat16 [512, 128, 1152], P(('clip', 'seq')), parts along dimension 0
- temporal_keys_grad: bfloat16 [512, 128, 1152], P(('clip', 'seq')), parts along dimension 0
- temporal_values_grad: bfloat16 [512, 128, 1152], P(('clip', 'seq')), parts along dimension 0
- cross_queries_grad: bfloat16 [512, 128, 1152], P(('clip', 'seq')), parts along dimension 0
- text_kv_grad: float32 [640, 2304], P('clip', 'seq'), parts along dimension 0
There are 4 independent parts, one for each index of `clip`. A program takes and returns all parts, laid end to end along the dimension named above; each array names one. Nothing has to cross between parts.
All inputs are finite; a program needn't handle non-finite values.
Results may differ from a plain program's by a relative error of at most 0.012.
The roundings to bfloat16 on the way count: a program that leaves them out, or rounds other values in their place, can miss the bound.
Values may be sent and summed in bfloat16 or wider, within the bound.
A program may use at most 64 MiB of HBM per device.

v0:
```python
import math

import jax
import jax.numpy as jnp
from jax import lax
from jax.sharding import Mesh
from jax.sharding import PartitionSpec as P

HEADS = 16
SEQ = ("seq_0", "seq_1", "seq_2")
CLIP_SEQ = ("clip", "seq_0", "seq_1", "seq_2")


def in_blocks(array, dim, count):
    before, after = (array.shape[:dim], array.shape[dim + 1 :])
    return jnp.moveaxis(array.reshape(*before, count, -1, *after), dim, 0)


def edges_of(length, count):
    turn = length // count
    if turn >= 8:
        turn -= turn % 8
    return [turn * k for k in range(1, count)]


def joined_along(blocks, dim):
    shape = list(blocks.shape[1:])
    shape[dim] *= blocks.shape[0]
    return jnp.moveaxis(blocks, 0, dim).reshape(shape)


def cut_exchange(array, axis, pieces, split_dim, concat_dim):
    blocks = in_blocks(array, split_dim, lax.axis_size(axis))
    split_at = max(range(1, max(2, blocks.ndim - 1)), key=lambda d: blocks.shape[d])
    outs = []
    for section in jnp.split(blocks, edges_of(blocks.shape[split_at], pieces), axis=split_at):
        if section.size:
            outs.append(lax.all_to_all(section, axis, split_axis=0, concat_axis=0, tiled=True))
    return joined_along(jnp.concatenate(outs, axis=split_at), concat_dim)


def own_block(blocks, axes, turns):
    inside = blocks.shape[1:]
    blocks = blocks.reshape(*(lax.axis_size(a) for a in axes), *inside)
    blocks = jnp.moveaxis(blocks, turns, range(len(axes))).reshape(-1, *inside)
    for k in turns:
        blocks = lax.psum_scatter(blocks, axes[k], scatter_dimension=0, tiled=True)
    return blocks[0]


def sum_by_axis(array, axes, turns, dim):
    count = lax.axis_size(axes)
    return own_block(in_blocks(array, dim, count), axes, turns)


def attend_back(queries, targets, values, cotangent, keep, scale):
    scores = (
        jnp.einsum("mhe,nhe->hmn", queries, targets, preferred_element_type=jnp.float32) * scale
    )
    if keep is not None:
        scores = jnp.where(keep, scores, -1e30)
    highest_score = jnp.max(scores, axis=-1, keepdims=True)
    expo = jnp.exp(scores - highest_score)
    weights = expo / jnp.sum(expo, axis=-1, keepdims=True)
    rounded = weights.astype(jnp.bfloat16)
    output = jnp.einsum("hmn,nhe->mhe", rounded, values, preferred_element_type=jnp.float32)
    deltas = jnp.sum(cotangent.astype(jnp.float32) * output, axis=-1)
    grad_values = jnp.einsum("hmn,mhe->nhe", rounded, cotangent, preferred_element_type=jnp.float32)
    products = jnp.einsum("mhe,nhe->hmn", cotangent, values, preferred_element_type=jnp.float32)
    sloped = (weights * (products - jnp.transpose(deltas)[:, :, None]) * scale).astype(jnp.bfloat16)
    grad_queries = jnp.einsum("hmn,nhe->mhe", sloped, targets, preferred_element_type=jnp.float32)
    grad_targets = jnp.einsum("hmn,mhe->nhe", sloped, queries, preferred_element_type=jnp.float32)
    return (grad_queries, grad_targets, grad_values)


def local(
    temporal_queries,
    temporal_keys,
    temporal_values,
    temporal_cotangent,
    cross_queries,
    cross_cotangent,
    text_keys,
    text_values,
    text_length,
):
    frames_dev, positions, width = temporal_queries.shape
    head_dim = width // HEADS
    scale = 1.0 / math.sqrt(head_dim)
    text_rows = text_keys.shape[0]
    moved = (
        cut_exchange(temporal_queries.reshape(frames_dev, positions * width), SEQ, 2, 1, 0),
        cut_exchange(temporal_keys.reshape(frames_dev, positions * width), SEQ, 2, 1, 0),
        cut_exchange(temporal_values.reshape(frames_dev, positions * width), SEQ, 2, 1, 0),
        cut_exchange(temporal_cotangent.reshape(frames_dev, positions * width), SEQ, 2, 1, 0),
    )
    all_frames = moved[0].shape[0]
    grads = attend_back(
        moved[0].reshape(all_frames, -1, head_dim),
        moved[1].reshape(all_frames, -1, head_dim),
        moved[2].reshape(all_frames, -1, head_dim),
        moved[3].reshape(all_frames, -1, head_dim),
        None,
        scale,
    )
    keep = (jnp.arange(text_rows, dtype=jnp.int32) < text_length[0])[None, None, :]
    token_rows = frames_dev * positions
    text_grads = attend_back(
        cross_queries.reshape(token_rows, HEADS, head_dim),
        text_keys.reshape(text_rows, HEADS, head_dim),
        text_values.reshape(text_rows, HEADS, head_dim),
        cross_cotangent.reshape(token_rows, HEADS, head_dim),
        keep,
        scale,
    )
    partial_value = jnp.concatenate([text_grads[1], text_grads[2]], axis=2).reshape(
        text_rows, 2 * width
    )
    shared = sum_by_axis(partial_value, SEQ, (2, 1, 0), 1)
    cross_grad = text_grads[0].reshape(frames_dev, positions, width).astype(jnp.bfloat16)
    return (
        lax.all_to_all(
            grads[0].astype(jnp.bfloat16).reshape(all_frames, -1),
            SEQ,
            split_axis=0,
            concat_axis=1,
            tiled=True,
        ).reshape(frames_dev, positions, width),
        lax.all_to_all(
            grads[1].astype(jnp.bfloat16).reshape(all_frames, -1),
            SEQ,
            split_axis=0,
            concat_axis=1,
            tiled=True,
        ).reshape(frames_dev, positions, width),
        lax.all_to_all(
            grads[2].astype(jnp.bfloat16).reshape(all_frames, -1),
            SEQ,
            split_axis=0,
            concat_axis=1,
            tiled=True,
        ).reshape(frames_dev, positions, width),
        cross_grad,
        shared,
    )


def solution(mesh):
    torus = Mesh(
        mesh.devices.reshape(mesh.shape["clip"], 2, 16, 4), ("clip", "seq_0", "seq_1", "seq_2")
    )
    in_specs = (
        P(CLIP_SEQ, None, None),
        P(CLIP_SEQ, None, None),
        P(CLIP_SEQ, None, None),
        P(CLIP_SEQ, None, None),
        P(CLIP_SEQ, None, None),
        P(CLIP_SEQ, None, None),
        P("clip", None),
        P("clip", None),
        P("clip"),
    )
    out_specs = (
        P(CLIP_SEQ, None, None),
        P(CLIP_SEQ, None, None),
        P(CLIP_SEQ, None, None),
        P(CLIP_SEQ, None, None),
        P("clip", SEQ),
    )
    return jax.shard_map(local, mesh=torus, in_specs=in_specs, out_specs=out_specs, check_vma=False)
```

profile of v0, /device:TPU:1, one launch (start us, length us, event | category | flops | bytes accessed | tf_op | source)
XLA Modules:
  0.0 342.0 jit_solution(3944279373181887906)
XLA Ops:
  7.7 1.7 reduce.2
  9.4 1.1 reshape.101
  10.5 23.1 %all-to-all-start = ((bf16[128,2,576]{2,1,0:T(2,128)(2,1)}), bf16[128,2,576]{2,1,0:T(2,128)(2,1)S(1)}, u32[]{:S(2)}, u32[]{:S(2)}) async-start(bf16[128,2,576]{2,1,0:T(2,128)(2,1)} %reshape.101), calls=%async_computation | async-start | bytes 655360 | tf_op jit(solution)/shard_map/all_to_all | solution.py:38
  34.4 1.0 reshape.103
  35.4 24.4 %all-to-all-done = bf16[128,2,576]{2,1,0:T(2,128)(2,1)S(1)} async-done(((bf16[128,2,576]{2,1,0:T(2,128)(2,1)}), bf16[128,2,576]{2,1,0:T(2,128)(2,1)S(1)}, u32[]{:S(2)}, u32[]{:S(2)}) %all-to-all-start) | async-done | bytes 294944 | tf_op jit(solution)/shard_map/all_to_all | solution.py:38
  59.8 6.8 %all-to-all-start.1 = ((bf16[128,2,576]{2,1,0:T(2,128)(2,1)}), bf16[128,2,576]{2,1,0:T(2,128)(2,1)S(1)}, u32[]{:S(2)}, u32[]{:S(2)}) async-start(bf16[128,2,576]{2,1,0:T(2,128)(2,1)} %reshape.103), calls=%async_computation.1 | async-start | bytes 655360 | tf_op jit(solution)/shard_map/all_to_all | solution.py:38
  67.4 1.1 reshape.99
  68.5 22.4 %all-to-all-done.1 = bf16[128,2,576]{2,1,0:T(2,128)(2,1)S(1)} async-done(((bf16[128,2,576]{2,1,0:T(2,128)(2,1)}), bf16[128,2,576]{2,1,0:T(2,128)(2,1)S(1)}, u32[]{:S(2)}, u32[]{:S(2)}) %all-to-all-start.1) | async-done | bytes 294944 | tf_op jit(solution)/shard_map/all_to_all | solution.py:38
  90.9 8.4 %all-to-all-start.3 = ((bf16[128,2,576]{2,1,0:T(2,128)(2,1)}), bf16[128,2,576]{2,1,0:T(2,128)(2,1)S(1)}, u32[]{:S(2)}, u32[]{:S(2)}) async-start(bf16[128,2,576]{2,1,0:T(2,128)(2,1)} %reshape.99), calls=%async_computation.3 | async-start | bytes 655360 | tf_op jit(solution)/shard_map/all_to_all | solution.py:38
  100.9 1.1 reshape.97
  102.9 1.7 fusion.29
  104.6 19.0 %all-to-all-done.3 = bf16[128,2,576]{2,1,0:T(2,128)(2,1)S(1)} async-done(((bf16[128,2,576]{2,1,0:T(2,128)(2,1)}), bf16[128,2,576]{2,1,0:T(2,128)(2,1)S(1)}, u32[]{:S(2)}, u32[]{:S(2)}) %all-to-all-start.3) | async-done | bytes 294944 | tf_op jit(solution)/shard_map/all_to_all | solution.py:38
  123.6 8.8 %all-to-all-start.2 = ((bf16[128,2,576]{2,1,0:T(2,128)(2,1)}), bf16[128,2,576]{2,1,0:T(2,128)(2,1)}, u32[]{:S(2)}, u32[]{:S(2)}) async-start(bf16[128,2,576]{2,1,0:T(2,128)(2,1)} %reshape.97), calls=%async_computation.2 | async-start | bytes 655360 | tf_op jit(solution)/shard_map/all_to_all | solution.py:38
  132.6 1.8 fusion.15
  136.8 1.7 pad_maximum_fusion
  138.5 2.5 reshape_reshape.19
  141.0 2.1 copy.97
  146.8 9.3 %all-to-all-done.2 = bf16[128,2,576]{2,1,0:T(2,128)(2,1)} async-done(((bf16[128,2,576]{2,1,0:T(2,128)(2,1)}), bf16[128,2,576]{2,1,0:T(2,128)(2,1)}, u32[]{:S(2)}, u32[]{:S(2)}) %all-to-all-start.2) | async-done | bytes 294944 | tf_op jit(solution)/shard_map/all_to_all | solution.py:38
  156.1 2.5 reshape.98
  161.9 1.1 reshape.105
  163.0 8.8 %all-to-all-start.4 = ((bf16[128,2,576]{2,1,0:T(2,128)(2,1)}), bf16[128,2,576]{2,1,0:T(2,128)(2,1)S(1)}, u32[]{:S(2)}, u32[]{:S(2)}) async-start(bf16[128,2,576]{2,1,0:T(2,128)(2,1)} %reshape.105), calls=%async_computation.4 | async-start | bytes 655360 | tf_op jit(solution)/shard_map/all_to_all | solution.py:122
  172.3 0.8 reduce.6
  173.4 1.1 reshape.109
  174.4 20.4 %all-to-all-done.4 = bf16[128,2,576]{2,1,0:T(2,128)(2,1)S(1)} async-done(((bf16[128,2,576]{2,1,0:T(2,128)(2,1)}), bf16[128,2,576]{2,1,0:T(2,128)(2,1)S(1)}, u32[]{:S(2)}, u32[]{:S(2)}) %all-to-all-start.4) | async-done | bytes 294944 | tf_op jit(solution)/shard_map/all_to_all | solution.py:122
  194.8 8.6 %all-to-all-start.6 = ((bf16[128,2,576]{2,1,0:T(2,128)(2,1)}), bf16[128,2,576]{2,1,0:T(2,128)(2,1)S(1)}, u32[]{:S(2)}, u32[]{:S(2)}) async-start(bf16[128,2,576]{2,1,0:T(2,128)(2,1)} %reshape.109), calls=%async_computation.6 | async-start | bytes 655360 | tf_op jit(solution)/shard_map/all_to_all | solution.py:136
  203.9 0.8 reduce.5
  204.9 1.1 reshape.107
  206.0 20.1 %all-to-all-done.6 = bf16[128,2,576]{2,1,0:T(2,128)(2,1)S(1)} async-done(((bf16[128,2,576]{2,1,0:T(2,128)(2,1)}), bf16[128,2,576]{2,1,0:T(2,128)(2,1)S(1)}, u32[]{:S(2)}, u32[]{:S(2)}) %all-to-all-start.6) | async-done | bytes 294944 | tf_op jit(solution)/shard_map/all_to_all | solution.py:136
  226.1 8.8 %all-to-all-start.5 = ((bf16[128,2,576]{2,1,0:T(2,128)(2,1)}), bf16[128,2,576]{2,1,0:T(2,128)(2,1)S(1)}, u32[]{:S(2)}, u32[]{:S(2)}) async-start(bf16[128,2,576]{2,1,0:T(2,128)(2,1)} %reshape.107), calls=%async_computation.5 | async-start | bytes 655360 | tf_op jit(solution)/shard_map/all_to_all | solution.py:129
  235.7 67.1 %reduce-scatter.6.cloned.1.call-done = f32[2,160,18]{1,2,0:T(8,128)} async-done(((f32[32,160,18]{1,2,0:T(8,128)}), f32[2,160,18]{1,2,0:T(8,128)}) %reduce-scatter.6.cloned.1.call-update) | async-done | bytes 23056 | tf_op jit(solution)/shard_map/reduce_scatter | solution.py:47
  303.2 0.9 copy.98
  307.9 27.6 %reduce-scatter.8.cloned.1.call-done = f32[1,160,18]{1,2,0:T(8,128)} async-done(((f32[2,160,18]{1,2,0:T(8,128)}), f32[1,160,18]{1,2,0:T(8,128)}) %reduce-scatter.8.cloned.1.call-update) | async-done | bytes 11536 | tf_op jit(solution)/shard_map/reduce_scatter | solution.py:47
  (76 shorter events, 19.6 us)
Async XLA Ops:
  7.2 26.4 %copy-start.12 = (bf16[1,128,1152]{2,1,0:T(8,128)(2,1)S(1)}, bf16[1,128,1152]{2,1,0:T(8,128)(2,1)}, u32[]{:S(2)}) copy-start(bf16[1,128,1152]{2,1,0:T(8,128)(2,1)} %param.10) | copy-start | bytes 884740
  10.5 56.1 %copy-start.13 = (bf16[1,128,1152]{2,1,0:T(8,128)(2,1)S(1)}, bf16[1,128,1152]{2,1,0:T(8,128)(2,1)}, u32[]{:S(2)}) copy-start(bf16[1,128,1152]{2,1,0:T(8,128)(2,1)} %param.11) | copy-start | bytes 884740
  10.5 49.3 %all-to-all-start = ((bf16[128,2,576]{2,1,0:T(2,128)(2,1)}), bf16[128,2,576]{2,1,0:T(2,128)(2,1)S(1)}, u32[]{:S(2)}, u32[]{:S(2)}) async-start(bf16[128,2,576]{2,1,0:T(2,128)(2,1)} %reshape.101), calls=%async_computation | async-start | bytes 655360 | tf_op jit(solution)/shard_map/all_to_all | solution.py:38
  35.4 64.7 %copy-start.14 = (bf16[1,128,1152]{2,1,0:T(8,128)(2,1)S(1)}, bf16[1,128,1152]{2,1,0:T(8,128)(2,1)}, u32[]{:S(2)}) copy-start(bf16[1,128,1152]{2,1,0:T(8,128)(2,1)} %param.12) | copy-start | bytes 884740
  59.8 31.1 %all-to-all-start.1 = ((bf16[128,2,576]{2,1,0:T(2,128)(2,1)}), bf16[128,2,576]{2,1,0:T(2,128)(2,1)S(1)}, u32[]{:S(2)}, u32[]{:S(2)}) async-start(bf16[128,2,576]{2,1,0:T(2,128)(2,1)} %reshape.103), calls=%async_computation.1 | async-start | bytes 655360 | tf_op jit(solution)/shard_map/all_to_all | solution.py:38
  67.4 34.5 %copy-start.10 = (bf16[1,128,1152]{2,1,0:T(8,128)(2,1)S(1)}, bf16[1,128,1152]{2,1,0:T(8,128)(2,1)}, u32[]{:S(2)}) copy-start(bf16[1,128,1152]{2,1,0:T(8,128)(2,1)} %param.13) | copy-start | bytes 884740
  68.5 33.7 %copy-start.11 = (bf16[1,128,1152]{2,1,0:T(8,128)(2,1)S(1)}, bf16[1,128,1152]{2,1,0:T(8,128)(2,1)}, u32[]{:S(2)}) copy-start(bf16[1,128,1152]{2,1,0:T(8,128)(2,1)} %param.14) | copy-start | bytes 884740
  90.9 11.2 %copy-start.4 = (bf16[128,2,576]{2,1,0:T(2,128)(2,1)}, bf16[128,2,576]{2,1,0:T(2,128)(2,1)S(1)}, u32[]{:S(2)}) copy-start(bf16[128,2,576]{2,1,0:T(2,128)(2,1)S(1)} %all-to-all-done.1) | copy-start | bytes 884740
  90.9 32.7 %all-to-all-start.3 = ((bf16[128,2,576]{2,1,0:T(2,128)(2,1)}), bf16[128,2,576]{2,1,0:T(2,128)(2,1)S(1)}, u32[]{:S(2)}, u32[]{:S(2)}) async-start(bf16[128,2,576]{2,1,0:T(2,128)(2,1)} %reshape.99), calls=%async_computation.3 | async-start | bytes 655360 | tf_op jit(solution)/shard_map/all_to_all | solution.py:38
  99.4 3.0 copy-start.8
  100.9 1.8 copy-start.9
  102.6 2.0 copy-start.2
  123.6 10.8 %copy-start.6 = (bf16[128,2,576]{2,1,0:T(2,128)(2,1)}, bf16[128,2,576]{2,1,0:T(2,128)(2,1)S(1)}, u32[]{:S(2)}) copy-start(bf16[128,2,576]{2,1,0:T(2,128)(2,1)S(1)} %all-to-all-done.3) | copy-start | bytes 884740
  123.6 32.5 %all-to-all-start.2 = ((bf16[128,2,576]{2,1,0:T(2,128)(2,1)}), bf16[128,2,576]{2,1,0:T(2,128)(2,1)}, u32[]{:S(2)}, u32[]{:S(2)}) async-start(bf16[128,2,576]{2,1,0:T(2,128)(2,1)} %reshape.97), calls=%async_computation.2 | async-start | bytes 655360 | tf_op jit(solution)/shard_map/all_to_all | solution.py:38
  132.4 102.6 %reduce-scatter.4.cloned.1.call-start = ((), (), s32[]{:S(2)}) async-start(), calls=%async_computation.10 | async-start | bytes 3932160 | tf_op jit(solution)/shard_map/reduce_scatter | solution.py:47
  132.6 1.8 copy-start.15
  134.9 0.8 copy-start
  143.1 1.2 copy-start.5
  143.7 1.9 copy-start.7
  163.0 31.8 %all-to-all-start.4 = ((bf16[128,2,576]{2,1,0:T(2,128)(2,1)}), bf16[128,2,576]{2,1,0:T(2,128)(2,1)S(1)}, u32[]{:S(2)}, u32[]{:S(2)}) async-start(bf16[128,2,576]{2,1,0:T(2,128)(2,1)} %reshape.105), calls=%async_computation.4 | async-start | bytes 655360 | tf_op jit(solution)/shard_map/all_to_all | solution.py:122
  194.8 31.3 %all-to-all-start.6 = ((bf16[128,2,576]{2,1,0:T(2,128)(2,1)}), bf16[128,2,576]{2,1,0:T(2,128)(2,1)S(1)}, u32[]{:S(2)}, u32[]{:S(2)}) async-start(bf16[128,2,576]{2,1,0:T(2,128)(2,1)} %reshape.109), calls=%async_computation.6 | async-start | bytes 655360 | tf_op jit(solution)/shard_map/all_to_all | solution.py:136
  204.7 98.1 %copy-start.1 = (bf16[16,128,160]{1,2,0:T(8,128)(2,1)S(1)}, bf16[16,128,160]{1,2,0:T(8,128)(2,1)}, u32[]{:S(2)}) copy-start(bf16[16,128,160]{1,2,0:T(8,128)(2,1)} %copy-done) | copy-start | bytes 1966084
  204.7 98.1 %copy-start.3 = (bf16[160,1152]{0,1:T(8,128)(2,1)S(1)}, bf16[160,1152]{0,1:T(8,128)(2,1)}, u32[]{:S(2)}) copy-start(bf16[160,1152]{0,1:T(8,128)(2,1)} %copy-done.2) | copy-start | bytes 1105924
  226.1 80.5 %all-to-all-start.5 = ((bf16[128,2,576]{2,1,0:T(2,128)(2,1)}), bf16[128,2,576]{2,1,0:T(2,128)(2,1)S(1)}, u32[]{:S(2)}, u32[]{:S(2)}) async-start(bf16[128,2,576]{2,1,0:T(2,128)(2,1)} %reshape.107), calls=%async_computation.5 | async-start | bytes 655360 | tf_op jit(solution)/shard_map/all_to_all | solution.py:129
  234.9 67.9 %reduce-scatter.6.cloned.1.call-start = ((), (), s32[]{:S(2)}) async-start(), calls=%async_computation.11 | async-start | bytes 835584 | tf_op jit(solution)/shard_map/reduce_scatter | solution.py:47
  235.7 99.8 %reduce-scatter.8.cloned.1.call-start = ((), (), s32[]{:S(2)}) async-start(), calls=%async_computation.12 | async-start | bytes 73728 | tf_op jit(solution)/shard_map/reduce_scatter | solution.py:47
Sparse Core Ops, SparseCore 0:
  143.3 52.7 reduce-scatter.3
  238.5 64.2 reduce-scatter.5
  306.1 29.2 reduce-scatter.7
where the time goes:
time: 343 us; the launch traced here: 342 us
  waiting for transfers between devices  211 us (62%)
  starting transfers between devices  73.6 us (21%)
  local copies, waits for them, and re-layouts  26.4 us (8%)
  between operations  14.9 us (4%)
  other arithmetic  8.26 us (2%)
  matrix products  7.9 us (2%)
    reduce_scatter x3, waiting for transfers between devices, own_block(): blocks = lax.psum_scatter(blocks, axes[k], scatter_dimension=0, tiled=True)  94.7 us
    all_to_all x4, waiting for transfers between devices, cut_exchange(): lax.all_to_all(section, axis, split_axis=0, concat_axis=0, tiled=True)  75.1 us
    all_to_all x4, starting transfers between devices, cut_exchange(): lax.all_to_all(section, axis, split_axis=0, concat_axis=0, tiled=True)  47.1 us
    all_to_all x1, waiting for transfers between devices, local(): lax.all_to_all(grads[0].astype(jnp.bfloat16).reshape(all_frames, -1), SEQ...  20.4 us
    all_to_all x1, waiting for transfers between devices, local(): lax.all_to_all(grads[2].astype(jnp.bfloat16).reshape(all_frames, -1), SEQ...  20.1 us
    unnamed x55, local copies, waits for them, and re-layouts  18.1 us
    all_to_all x1, starting transfers between devices, local(): lax.all_to_all(grads[0].astype(jnp.bfloat16).reshape(all_frames, -1), SEQ...  8.85 us
    all_to_all x1, starting transfers between devices, local(): lax.all_to_all(grads[1].astype(jnp.bfloat16).reshape(all_frames, -1), SEQ...  8.79 us
  transfers between devices with their start and end apart: 10, of which 8 were waited for; matrix products, arithmetic and copies ran while one was open for 11% of the time, Pallas kernels for 0%

commit v1 on v0

v1 whole, which is shorter than its diff:
```python
import math

import jax
import jax.numpy as jnp
from jax import lax
from jax.experimental import pallas as pl
from jax.experimental.pallas import tpu as pltpu
from jax.sharding import Mesh
from jax.sharding import PartitionSpec as P

HEADS = 16
HEAD_DIM = 72
WIDTH = HEADS * HEAD_DIM
POS = 128
TEXT = 160
NZ = 16
NX = 4
NPL = 8
SCALE = 1.0 / math.sqrt(HEAD_DIM)
CLIP_SEQ = ("clip", "seq_0", "seq_1", "seq_2")
SEQ = ("seq_0", "seq_1", "seq_2")
MESH = pl.DeviceIdType.MESH
BF = jnp.bfloat16
F32 = jnp.float32

IN_CHUNKS = ((0, 640), (640, 512))
HEAD_CHUNKS = ((0, 8), (8, 16))
OUT_CHUNKS = ((0, 512), (512, 640))
DISTANCES = (8, 7, 9, 6, 10, 5, 11, 4, 12, 3, 13, 2, 14, 1, 15)
TEXT_ROWS = TEXT // NX
HALF = 640


def window(head):
    low = HEAD_DIM * head // 128 * 128
    return low, -(-HEAD_DIM * (head + 1) // 128) * 128


def head_mask(head):
    low, high = window(head)
    lane = lax.broadcasted_iota(jnp.int32, (1, high - low), 1) + low
    inside = (lane >= HEAD_DIM * head) & (lane < HEAD_DIM * (head + 1))
    return jnp.where(inside, 1.0, 0.0).astype(BF)


def across(a, b):
    return lax.dot_general(a, b, (((1,), (1,)), ((), ())), preferred_element_type=F32)


def down(a, b):
    return lax.dot_general(a, b, (((0,), (0,)), ((), ())), preferred_element_type=F32)


def head_back(q, k, v, g, mask, keep):
    kz, vz, qz, gz = k * mask, v * mask, q * mask, g * mask
    scores = across(kz, q) * SCALE
    if keep is not None:
        scores = jnp.where(keep, scores, -1e30)
    expo = jnp.exp(scores - jnp.max(scores, axis=0, keepdims=True))
    weights = expo * (1.0 / jnp.sum(expo, axis=0, keepdims=True))
    rounded = weights.astype(BF)
    products = across(vz, g)
    delta = jnp.sum(rounded.astype(F32) * products, axis=0, keepdims=True)
    slopes = (weights * (products - delta) * SCALE).astype(BF)
    grad_v = jnp.dot(rounded, gz, preferred_element_type=F32)
    grad_k = jnp.dot(slopes, qz, preferred_element_type=F32)
    grad_q = down(slopes, kz)
    return grad_q, grad_k, grad_v


class Tiles:
    def __init__(self, store):
        self.open, self.store = {}, store

    def add(self, head, value):
        low, high = window(head)
        for t in range(low // 128, high // 128):
            part = value[:, 128 * t - low : 128 * t - low + 128]
            self.open[t] = part if t not in self.open else self.open[t] + part
            if HEAD_DIM * (head + 1) >= 128 * (t + 1):
                self.store(t, self.open.pop(t))


def kernel(
    tq, tk, tv, tg, cq, cg, xk, xv, length,
    oq, ok, ov, ocq, otext,
    zbuf, pout, pbuf, gbuf, qbuf, zout, tall, tpart, rs1, rs2out, rs2, rs3out, rs3,
    zs, zr, ps, pr, qs, qr, ws, wr, ts, tr,
):
    y, z, x = lax.axis_index("seq_0"), lax.axis_index("seq_1"), lax.axis_index("seq_2")
    me = y * NX + x
    ins, outs = (tq, tk, tv, tg), (oq, ok, ov)

    def z_peer(k):
        return lax.rem(z + k, NZ)

    def plane_peer(k):
        return lax.rem(y + k // NX, 2), lax.rem(x + k % NX, NX)

    def in_plane(k):
        py, px = plane_peer(k)
        return {"seq_0": py, "seq_2": px}

    barrier = pltpu.get_barrier_semaphore()
    for k in range(1, NZ):
        pl.semaphore_signal(barrier, 1, device_id={"seq_1": z_peer(k)}, device_id_type=MESH)
    for k in range(1, NPL):
        pl.semaphore_signal(barrier, 1, device_id=in_plane(k), device_id_type=MESH)
    pl.semaphore_wait(barrier, NZ - 1 + NPL - 1)

    def send(src, dst, send_sem, recv_sem, device):
        pltpu.make_async_remote_copy(
            src_ref=src, dst_ref=dst, send_sem=send_sem, recv_sem=recv_sem, device_id=device, device_id_type=MESH
        ).start()

    def wait_for(ref, sem):
        pltpu.make_async_copy(ref, ref, sem).wait()

    for c, (low, size) in enumerate(IN_CHUNKS):
        lanes = pl.ds(low, size)
        for a in range(4):
            for k in DISTANCES:
                peer = z_peer(k)
                send(ins[a].at[peer, :, lanes], zbuf.at[a, z, :, lanes], zs.at[c, a], zr.at[c, a], {"seq_1": peer})
    for a in range(4):
        zbuf[a, z] = ins[a][z]

    text_rows = lax.broadcasted_iota(jnp.int32, (TEXT, POS), 0)
    keep = text_rows < length[0]

    def put_cross(t, value):
        ocq[:, 128 * t : 128 * t + 128] = value.astype(BF)

    def put_text(kind):
        def put(t, value):
            tpart[kind, :, 128 * t : 128 * t + 128] = value

        return put

    sums = (Tiles(put_cross), Tiles(put_text(0)), Tiles(put_text(1)))
    for h in range(HEADS):
        low, high = window(h)
        grads = head_back(cq[:, low:high], xk[:, low:high], xv[:, low:high], cg[:, low:high], head_mask(h), keep)
        for s, grad in zip(sums, grads, strict=True):
            s.add(h, grad)

    for k in range(1, NPL):
        py, px = plane_peer(k)
        rows, lanes = pl.ds(pl.multiple_of(px * TEXT_ROWS, 8), TEXT_ROWS), pl.ds(pl.multiple_of(py * 512, 128), HALF)
        send(tpart.at[:, rows, lanes], rs1.at[me], ts.at[0], tr.at[0], in_plane(k))
    own_rows, own_lanes = pl.ds(pl.multiple_of(x * TEXT_ROWS, 8), TEXT_ROWS), pl.ds(pl.multiple_of(y * 512, 128), HALF)
    rs1[me] = tpart[:, own_rows, own_lanes]

    def hand_on(c):
        low, size = IN_CHUNKS[c]
        lanes = pl.ds(low, size)
        for a in range(4):
            wait_for(zbuf.at[a, pl.ds(0, NZ - 1), :, lanes], zr.at[c, a])
            for t in range(low, low + size, 128):
                for f in range(NZ):
                    tall[t // 128, pl.ds(f, NPL, stride=NZ), :] = zbuf[a, f, :, t : t + 128].astype(F32)
                for j in range(NPL):
                    pout[a, j, :, t : t + 128] = tall[t // 128, NZ * j : NZ * j + NZ, :].astype(BF)
            for k in range(1, NPL):
                py, px = plane_peer(k)
                send(pout.at[a, py * NX + px, :, lanes], pbuf.at[a, me, :, lanes], ps.at[c, a], pr.at[c, a], in_plane(k))
            pbuf[a, me, :, low : low + size] = pout[a, me, :, low : low + size]

    def put_temporal(a):
        def put(t, value):
            gbuf[a, :, :, 128 * t : 128 * t + 128] = value.astype(BF).reshape(NPL, NZ, 128)

        return put

    temporal = tuple(Tiles(put_temporal(a)) for a in range(3))

    def attend(c):
        low, size = IN_CHUNKS[c]
        for a in range(4):
            wait_for(pbuf.at[a, pl.ds(0, NPL - 1), :, pl.ds(low, size)], pr.at[c, a])
        for h in range(*HEAD_CHUNKS[c]):
            lo, hi = window(h)
            q, k, v, g = (pbuf[a, :, :, lo:hi].reshape(POS, hi - lo) for a in range(4))
            for s, grad in zip(temporal, head_back(q, k, v, g, head_mask(h), None), strict=True):
                s.add(h, grad)

    def give_back(c):
        low, size = OUT_CHUNKS[c]
        lanes = pl.ds(low, size)
        for a in range(3):
            for k in range(1, NPL):
                py, px = plane_peer(k)
                send(gbuf.at[a, py * NX + px, :, lanes], qbuf.at[a, me, :, lanes], qs.at[c, a], qr.at[c, a], in_plane(k))
            qbuf[a, me, :, low : low + size] = gbuf[a, me, :, low : low + size]

    def deliver(c):
        low, size = OUT_CHUNKS[c]
        lanes = pl.ds(low, size)
        for a in range(3):
            wait_for(qbuf.at[a, pl.ds(0, NPL - 1), :, lanes], qr.at[c, a])
            for t in range(low, low + size, 128):
                for j in range(NPL):
                    tall[t // 128, pl.ds(j, NZ, stride=NPL), :] = qbuf[a, j, :, t : t + 128].astype(F32)
                for f in range(NZ):
                    zout[a, f, :, t : t + 128] = tall[t // 128, NPL * f : NPL * f + NPL, :].astype(BF)
            for k in DISTANCES:
                peer = z_peer(k)
                send(zout.at[a, peer, :, lanes], outs[a].at[z, :, lanes], ws.at[c, a], wr.at[c, a], {"seq_1": peer})
            outs[a][z, :, low : low + size] = zout[a, z, :, low : low + size]

    hand_on(0)

    wait_for(rs1.at[pl.ds(0, NPL - 1)], tr.at[0])
    for kind in range(2):
        total = rs1[0, kind]
        for j in range(1, NPL):
            total = total + rs1[j, kind]
        for i in range(HEADS // 2):
            first, second = (total[:, s : s + HEAD_DIM] for s in (HEAD_DIM * i, HEAD_DIM * i + 64))
            block = jnp.where(y == 0, first, second)
            rs2out[2 * i + kind] = jnp.pad(block, ((0, 0), (0, 128 - HEAD_DIM))).astype(BF)
    for k in DISTANCES:
        peer = z_peer(k)
        send(rs2out.at[peer], rs2.at[z], ts.at[1], tr.at[1], {"seq_1": peer})
    rs2[z] = rs2out[z]

    attend(0)
    give_back(0)
    hand_on(1)
    deliver(0)

    wait_for(rs2.at[pl.ds(0, NZ - 1)], tr.at[1])
    total = rs2[0].astype(F32)
    for f in range(1, NZ):
        total = total + rs2[f].astype(F32)
    columns = HEAD_DIM // NX
    for j in range(NX):
        rs3out[j] = jnp.pad(total[:, columns * j : columns * j + columns], ((0, 0), (0, 128 - columns)))
    for k in range(1, NX):
        _, px = plane_peer(k)
        send(rs3out.at[px], rs3.at[x], ts.at[2], tr.at[2], in_plane(k))
    rs3[x] = rs3out[x]

    attend(1)
    give_back(1)
    deliver(1)

    wait_for(rs3.at[pl.ds(0, NX - 1)], tr.at[2])
    for j in range(NX):
        otext[TEXT_ROWS * j : TEXT_ROWS * j + TEXT_ROWS, :] = rs3[j]

    for c in range(2):
        lanes_in, lanes_out = pl.ds(*IN_CHUNKS[c]), pl.ds(*OUT_CHUNKS[c])
        for a in range(4):
            wait_for(zbuf.at[a, pl.ds(0, NZ - 1), :, lanes_in], zs.at[c, a])
            wait_for(pout.at[a, pl.ds(0, NPL - 1), :, lanes_in], ps.at[c, a])
        for a in range(3):
            wait_for(gbuf.at[a, pl.ds(0, NPL - 1), :, lanes_out], qs.at[c, a])
            wait_for(zout.at[a, pl.ds(0, NZ - 1), :, lanes_out], ws.at[c, a])
            wait_for(outs[a].at[pl.ds(0, NZ - 1), :, lanes_out], wr.at[c, a])
    wait_for(rs1.at[pl.ds(0, NPL - 1)], ts.at[0])
    wait_for(rs2.at[pl.ds(0, NZ - 1)], ts.at[1])
    wait_for(rs3.at[pl.ds(0, NX - 1)], ts.at[2])


def local(tq, tk, tv, tg, cq, cg, xk, xv, length):
    blocks = [a.reshape(NZ, POS // NZ, WIDTH) for a in (tq, tk, tv, tg)]
    vmem, dma = pltpu.VMEM, pltpu.SemaphoreType.DMA
    block = jax.ShapeDtypeStruct((NZ, POS // NZ, WIDTH), BF)
    oq, ok, ov, ocq, otext = pl.pallas_call(
        kernel,
        name="attend_back",
        out_shape=(
            block,
            block,
            block,
            jax.ShapeDtypeStruct((POS, WIDTH), BF),
            jax.ShapeDtypeStruct((TEXT, 128), F32),
        ),
        in_specs=[pl.BlockSpec(memory_space=vmem)] * 8 + [pl.BlockSpec(memory_space=pltpu.SMEM)],
        out_specs=[pl.BlockSpec(memory_space=vmem)] * 5,
        scratch_shapes=[
            vmem((4, NZ, 8, WIDTH), BF),
            vmem((4, NPL, NZ, WIDTH), BF),
            vmem((4, NPL, NZ, WIDTH), BF),
            vmem((3, NPL, NZ, WIDTH), BF),
            vmem((3, NPL, NZ, WIDTH), BF),
            vmem((3, NZ, 8, WIDTH), BF),
            vmem((WIDTH // 128, POS, 128), F32),
            vmem((2, TEXT, WIDTH), F32),
            vmem((NPL, 2, TEXT_ROWS, HALF), F32),
            vmem((NZ, TEXT_ROWS, 128), BF),
            vmem((NZ, TEXT_ROWS, 128), BF),
            vmem((NX, TEXT_ROWS, 128), F32),
            vmem((NX, TEXT_ROWS, 128), F32),
            dma((2, 4)),
            dma((2, 4)),
            dma((2, 4)),
            dma((2, 4)),
            dma((2, 3)),
            dma((2, 3)),
            dma((2, 3)),
            dma((2, 3)),
            dma((3,)),
            dma((3,)),
        ],
        compiler_params=pltpu.CompilerParams(collective_id=0, has_side_effects=True),
    )(*blocks, cq.reshape(POS, WIDTH), cg.reshape(POS, WIDTH), xk, xv, length)
    whole = (1, POS, WIDTH)
    return oq.reshape(whole), ok.reshape(whole), ov.reshape(whole), ocq.reshape(whole), otext[:, : HEAD_DIM // NX]


def solution(mesh):
    torus = Mesh(mesh.devices.reshape(mesh.shape["clip"], 2, NZ, NX), CLIP_SEQ)
    tokens = P(CLIP_SEQ, None, None)
    return jax.shard_map(
        local,
        mesh=torus,
        in_specs=(tokens,) * 6 + (P("clip", None), P("clip", None), P("clip")),
        out_specs=(tokens,) * 4 + (P("clip", SEQ),),
        check_vma=False,
    )
```

time: 343 us -> 123 us (0.36)
  waiting for transfers between devices: 211 us -> 0 us
  Pallas kernels: 0 us -> 114 us
  starting transfers between devices: 73.6 us -> 0 us
  local copies, waits for them, and re-layouts: 26.4 us -> 6.17 us
  between operations: 14.9 us -> 1.29 us
  other arithmetic: 8.26 us -> 0 us
  matrix products: 7.9 us -> 0 us
    all_to_all x7 -> x0, waiting for transfers between devices: 116 us -> none  [the longest x4 75.1 us: cut_exchange(): lax.all_to_all(section, axis, split_axis=0, concat_axis=0, tiled=True)]
    pallas_call x0 -> x1, Pallas kernels: none -> 114 us  [local(): pl.pallas_call(kernel, name='attend_back', out_shape=(block, block, block...]
    reduce_scatter x3 -> x0, waiting for transfers between devices: 94.7 us -> none  [own_block(): blocks = lax.psum_scatter(blocks, axes[k], scatter_dimension=0, tiled=True)]
    all_to_all x7 -> x0, starting transfers between devices: 73.3 us -> none  [the longest x4 47.1 us: cut_exchange(): lax.all_to_all(section, axis, split_axis=0, concat_axis=0, tiled=True)]
    unnamed x55 -> x11, local copies, waits for them, and re-layouts: 18.1 us -> 6.17 us
    dot_general x10 -> x0, matrix products: 5.68 us -> none  [the longest x2 2.09 us: attend_back(): jnp.einsum('hmn,nhe->mhe', rounded, values, preferred_element_type=jnp.fl...]
    another operation x4 -> x0, other arithmetic: 4.06 us -> none  [in_blocks(): return jnp.moveaxis(array.reshape(*before, count, -1, *after), dim, 0)]
  transfers between devices with their start and end apart: 10 -> 0, of which waited for: 8 -> 0; matrix products, arithmetic and copies ran while one was open for 11% -> 0% of each run, Pallas kernels for 0% -> 0%
where the time goes in v1:
time: 123 us; the launch traced here: 122 us
  Pallas kernels  114 us (93%)
  local copies, waits for them, and re-layouts  6.17 us (5%)
  between operations  1.29 us (1%)
    pallas_call x1, Pallas kernels, local(): pl.pallas_call(kernel, name='attend_back', out_shape=(block, block, block...  114 us
    unnamed x11, local copies, waits for them, and re-layouts  6.17 us

profile of v1, /device:TPU:1, one launch (start us, length us, event | category | flops | bytes accessed | tf_op | source)
XLA Modules:
  0.0 121.6 jit_solution(2226722786552705756)
XLA Ops:
  1.3 114.1 %attend_back.1 = (bf16[16,8,1152]{2,1,0:T(8,128)(2,1)}, bf16[16,8,1152]{2,1,0:T(8,128)(2,1)}, bf16[16,8,1152]{2,1,0:T(8,128)(2,1)}, bf16[128,1152]{1,0:T(8,128)(2,1)}, f32[160,128]{1,0:T(8,128)}) custom-call(bf16[16,8,1152]{2,1,0:T(8,128)(2,1)} %bitcast.15, bf16[16,8,1152]{2,1,0:T(8,128)(2,1)} %bitcast.16, bf16[16,8,1152]{2,1,0:T(8,128)(2,1)} %bitcast.17, ...), custom_call_target="tpu_custom_call" | custom-call | tf_op jit(solution)/shard_map/attend_back/pallas_call | solution.py:270
  115.4 1.6 %copy.14 = f32[160,18]{0,1:T(8,128)} copy(f32[160,18]{1,0:T(8,128)} %bitcast.21) | data formatting | bytes 23040
  117.0 0.0 copy-start.2
  117.0 1.7 %copy.20 = bf16[1,128,1152]{2,1,0:T(8,128)(2,1)} copy(bf16[1,128,1152]{2,1,0:T(8,128)(2,1)} %bitcast.14) | data formatting | bytes 589824
  118.8 0.0 copy-done.2
  118.8 0.0 copy-start.1
  118.8 0.7 copy.21
  119.5 0.4 copy-done.1
  119.8 0.0 copy-start
  119.8 0.7 copy.22
  120.5 0.4 copy-done
  120.9 0.7 copy.23
Async XLA Ops:
  117.0 1.7 %copy-start.2 = (bf16[16,8,1152]{2,1,0:T(8,128)(2,1)S(1)}, bf16[16,8,1152]{2,1,0:T(8,128)(2,1)}, u32[]{:S(2)}) copy-start(bf16[16,8,1152]{2,1,0:T(8,128)(2,1)} %get-tuple-element.11) | copy-start | bytes 884740
  118.8 1.1 copy-start.1
  119.8 1.1 copy-start

commit v2 on v1

--- a/solution.py
+++ b/solution.py
@@ -14,6 +14,7 @@
 POS = 128
 TEXT = 160
 NZ = 16
+NP = NZ // 2
 NX = 4
 NPL = 8
 SCALE = 1.0 / math.sqrt(HEAD_DIM)
@@ -27,6 +28,7 @@
 HEAD_CHUNKS = ((0, 8), (8, 16))
 OUT_CHUNKS = ((0, 512), (512, 640))
 DISTANCES = (8, 7, 9, 6, 10, 5, 11, 4, 12, 3, 13, 2, 14, 1, 15)
+PAIR_DISTANCES = (4, 3, 5, 2, 6, 1, 7)
 TEXT_ROWS = TEXT // NX
 HALF = 640
 
@@ -68,6 +70,19 @@
     return grad_q, grad_k, grad_v
 
 
+def packed(block):
+    rows = [block[8 * r : 8 * r + 8] for r in range(5)]
+    last = [rows[4][:, :64], *(row[:, 64:] for row in rows), jnp.zeros((8, 24), F32)]
+    parts = ([rows[0][:, :64], rows[1][:, :64]], [rows[2][:, :64], rows[3][:, :64]], last)
+    return jnp.concatenate([jnp.concatenate(part, axis=1) for part in parts], axis=0)
+
+
+def unpacked(block):
+    rows = [block[8 * (r // 2) : 8 * (r // 2) + 8, 64 * (r % 2) : 64 * (r % 2) + 64] for r in range(5)]
+    rest = [block[16:24, 64 + 8 * r : 72 + 8 * r] for r in range(5)]
+    return jnp.concatenate([jnp.concatenate(pair, axis=1) for pair in zip(rows, rest, strict=True)], axis=0)
+
+
 class Tiles:
     def __init__(self, store):
         self.open, self.store = {}, store
@@ -84,11 +99,14 @@
 def kernel(
     tq, tk, tv, tg, cq, cg, xk, xv, length,
     oq, ok, ov, ocq, otext,
-    zbuf, pout, pbuf, gbuf, qbuf, zout, tall, tpart, rs1, rs2out, rs2, rs3out, rs3,
-    zs, zr, ps, pr, qs, qr, ws, wr, ts, tr,
+    zbuf, pout, pbuf, gbuf, qbuf, zout, tall, tpart, rs1, rsout, rsmine, rsin, rs2out, rs2, rs3out, rs3, cqb, cgb, xkb, xvb,
+    zs, zr, ps, pr, qs, qr, ws, wr, ts, tr, ls, os,
 ):
     y, z, x = lax.axis_index("seq_0"), lax.axis_index("seq_1"), lax.axis_index("seq_2")
     me = y * NX + x
+    parity, pair = lax.rem(z, 2), z // 2
+    turned = lax.rem(z + lax.rem(lax.axis_index("clip"), 2), 2)
+    partner = lax.rem(z + 1 - 2 * turned + NZ, NZ)
     ins, outs = (tq, tk, tv, tg), (oq, ok, ov)
 
     def z_peer(k):
@@ -106,6 +124,10 @@
         pl.semaphore_signal(barrier, 1, device_id={"seq_1": z_peer(k)}, device_id_type=MESH)
     for k in range(1, NPL):
         pl.semaphore_signal(barrier, 1, device_id=in_plane(k), device_id_type=MESH)
+    loads = [pltpu.make_async_copy(*pair, ls.at[i]) for i, pair in enumerate(((cq, cqb), (cg, cgb), (xk, xkb), (xv, xvb)))]
+    loads += [pltpu.make_async_copy(ins[a].at[z], zbuf.at[a, z], ls.at[4 + a]) for a in range(4)]
+    for copy in loads:
+        copy.start()
     pl.semaphore_wait(barrier, NZ - 1 + NPL - 1)
 
     def send(src, dst, send_sem, recv_sem, device):
@@ -122,8 +144,8 @@
             for k in DISTANCES:
                 peer = z_peer(k)
                 send(ins[a].at[peer, :, lanes], zbuf.at[a, z, :, lanes], zs.at[c, a], zr.at[c, a], {"seq_1": peer})
-    for a in range(4):
-        zbuf[a, z] = ins[a][z]
+    for copy in loads:
+        copy.wait()
 
     text_rows = lax.broadcasted_iota(jnp.int32, (TEXT, POS), 0)
     keep = text_rows < length[0]
@@ -140,7 +162,7 @@
     sums = (Tiles(put_cross), Tiles(put_text(0)), Tiles(put_text(1)))
     for h in range(HEADS):
         low, high = window(h)
-        grads = head_back(cq[:, low:high], xk[:, low:high], xv[:, low:high], cg[:, low:high], head_mask(h), keep)
+        grads = head_back(*(b[:, low:high] for b in (cqb, xkb, xvb, cgb)), head_mask(h), keep)
         for s, grad in zip(sums, grads, strict=True):
             s.add(h, grad)
 
@@ -206,48 +228,47 @@
             for k in DISTANCES:
                 peer = z_peer(k)
                 send(zout.at[a, peer, :, lanes], outs[a].at[z, :, lanes], ws.at[c, a], wr.at[c, a], {"seq_1": peer})
-            outs[a][z, :, low : low + size] = zout[a, z, :, low : low + size]
+            pltpu.make_async_copy(zout.at[a, z, :, lanes], outs[a].at[z, :, lanes], os.at[c, a]).start()
 
     hand_on(0)
 
     wait_for(rs1.at[pl.ds(0, NPL - 1)], tr.at[0])
-    for kind in range(2):
-        total = rs1[0, kind]
-        for j in range(1, NPL):
-            total = total + rs1[j, kind]
-        for i in range(HEADS // 2):
-            first, second = (total[:, s : s + HEAD_DIM] for s in (HEAD_DIM * i, HEAD_DIM * i + 64))
-            block = jnp.where(y == 0, first, second)
-            rs2out[2 * i + kind] = jnp.pad(block, ((0, 0), (0, 128 - HEAD_DIM))).astype(BF)
-    for k in DISTANCES:
-        peer = z_peer(k)
-        send(rs2out.at[peer], rs2.at[z], ts.at[1], tr.at[1], {"seq_1": peer})
-    rs2[z] = rs2out[z]
+    keys, values = (sum((rs1[j, kind] for j in range(1, NPL)), rs1[0, kind]) for kind in range(2))
+    rsmine[...] = jnp.where(parity == 0, keys, values)
+    rsout[...] = jnp.where(parity == 0, values, keys).astype(BF)
+    send(rsout, rsin, ts.at[1], tr.at[1], {"seq_1": partner})
 
     attend(0)
     give_back(0)
+    deliver(0)
     hand_on(1)
-    deliver(0)
-
-    wait_for(rs2.at[pl.ds(0, NZ - 1)], tr.at[1])
-    total = rs2[0].astype(F32)
-    for f in range(1, NZ):
-        total = total + rs2[f].astype(F32)
+
+    wait_for(rsin, tr.at[1])
+    rsmine[...] = rsmine[...] + rsin[...].astype(F32)
+    for i in range(NP):
+        first, second = (rsmine[:, s : s + HEAD_DIM] for s in (HEAD_DIM * i, HEAD_DIM * i + 64))
+        rs2out[i] = packed(jnp.where(y == 0, first, second)).astype(BF)
+    for k in PAIR_DISTANCES:
+        peer = lax.rem(pair + k, NP)
+        send(rs2out.at[peer], rs2.at[pair], ts.at[2], tr.at[2], {"seq_1": 2 * peer + parity})
+    rs2[pair] = rs2out[pair]
+
+    attend(1)
+    give_back(1)
+    deliver(1)
+
+    wait_for(rs2.at[pl.ds(0, NP - 1)], tr.at[2])
+    total = unpacked(sum((rs2[f].astype(F32) for f in range(1, NP)), rs2[0].astype(F32)))
     columns = HEAD_DIM // NX
     for j in range(NX):
         rs3out[j] = jnp.pad(total[:, columns * j : columns * j + columns], ((0, 0), (0, 128 - columns)))
     for k in range(1, NX):
         _, px = plane_peer(k)
-        send(rs3out.at[px], rs3.at[x], ts.at[2], tr.at[2], in_plane(k))
+        send(rs3out.at[px], rs3.at[x], ts.at[3], tr.at[3], in_plane(k))
     rs3[x] = rs3out[x]
 
-    attend(1)
-    give_back(1)
-    deliver(1)
-
-    wait_for(rs3.at[pl.ds(0, NX - 1)], tr.at[2])
-    for j in range(NX):
-        otext[TEXT_ROWS * j : TEXT_ROWS * j + TEXT_ROWS, :] = rs3[j]
+    wait_for(rs3.at[pl.ds(0, NX - 1)], tr.at[3])
+    otext[...] = jnp.transpose(rs3[...].reshape(TEXT, 128))[:columns, :]
 
     for c in range(2):
         lanes_in, lanes_out = pl.ds(*IN_CHUNKS[c]), pl.ds(*OUT_CHUNKS[c])
@@ -258,27 +279,40 @@
             wait_for(gbuf.at[a, pl.ds(0, NPL - 1), :, lanes_out], qs.at[c, a])
             wait_for(zout.at[a, pl.ds(0, NZ - 1), :, lanes_out], ws.at[c, a])
             wait_for(outs[a].at[pl.ds(0, NZ - 1), :, lanes_out], wr.at[c, a])
+            wait_for(outs[a].at[0, :, lanes_out], os.at[c, a])
     wait_for(rs1.at[pl.ds(0, NPL - 1)], ts.at[0])
-    wait_for(rs2.at[pl.ds(0, NZ - 1)], ts.at[1])
-    wait_for(rs3.at[pl.ds(0, NX - 1)], ts.at[2])
+    wait_for(rsin, ts.at[1])
+    wait_for(rs2.at[pl.ds(0, NP - 1)], ts.at[2])
+    wait_for(rs3.at[pl.ds(0, NX - 1)], ts.at[3])
+
+
+def move(count, *refs):
+    copies = [pltpu.make_async_copy(refs[i], refs[count + i], refs[2 * count].at[i]) for i in range(count)]
+    for copy in copies:
+        copy.start()
+    for copy in copies:
+        copy.wait()
 
 
 def local(tq, tk, tv, tg, cq, cg, xk, xv, length):
-    blocks = [a.reshape(NZ, POS // NZ, WIDTH) for a in (tq, tk, tv, tg)]
+    arrays = [a.reshape(NZ, POS // NZ, WIDTH) for a in (tq, tk, tv, tg)]
+    arrays += [cq.reshape(POS, WIDTH), cg.reshape(POS, WIDTH), xk, xv]
     vmem, dma = pltpu.VMEM, pltpu.SemaphoreType.DMA
+    anywhere = pl.BlockSpec(memory_space=pl.ANY)
     block = jax.ShapeDtypeStruct((NZ, POS // NZ, WIDTH), BF)
-    oq, ok, ov, ocq, otext = pl.pallas_call(
+    shapes = (
+        block,
+        block,
+        block,
+        jax.ShapeDtypeStruct((POS, WIDTH), BF),
+        jax.ShapeDtypeStruct((HEAD_DIM // NX, TEXT), F32),
+    )
+    grads = pl.pallas_call(
         kernel,
         name="attend_back",
-        out_shape=(
-            block,
-            block,
-            block,
-            jax.ShapeDtypeStruct((POS, WIDTH), BF),
-            jax.ShapeDtypeStruct((TEXT, 128), F32),
-        ),
-        in_specs=[pl.BlockSpec(memory_space=vmem)] * 8 + [pl.BlockSpec(memory_space=pltpu.SMEM)],
-        out_specs=[pl.BlockSpec(memory_space=vmem)] * 5,
+        out_shape=shapes,
+        in_specs=[pl.BlockSpec(memory_space=pltpu.HBM)] * 8 + [pl.BlockSpec(memory_space=pltpu.SMEM)],
+        out_specs=[anywhere] * 3 + [pl.BlockSpec(memory_space=vmem)] * 2,
         scratch_shapes=[
             vmem((4, NZ, 8, WIDTH), BF),
             vmem((4, NPL, NZ, WIDTH), BF),
@@ -289,10 +323,17 @@
             vmem((WIDTH // 128, POS, 128), F32),
             vmem((2, TEXT, WIDTH), F32),
             vmem((NPL, 2, TEXT_ROWS, HALF), F32),
-            vmem((NZ, TEXT_ROWS, 128), BF),
-            vmem((NZ, TEXT_ROWS, 128), BF),
+            vmem((TEXT_ROWS, HALF), BF),
+            vmem((TEXT_ROWS, HALF), F32),
+            vmem((TEXT_ROWS, HALF), BF),
+            vmem((NP, 24, 128), BF),
+            vmem((NP, 24, 128), BF),
             vmem((NX, TEXT_ROWS, 128), F32),
             vmem((NX, TEXT_ROWS, 128), F32),
+            vmem((POS, WIDTH), BF),
+            vmem((POS, WIDTH), BF),
+            vmem((TEXT, WIDTH), BF),
+            vmem((TEXT, WIDTH), BF),
             dma((2, 4)),
             dma((2, 4)),
             dma((2, 4)),
@@ -301,13 +342,27 @@
             dma((2, 3)),
             dma((2, 3)),
             dma((2, 3)),
-            dma((3,)),
-            dma((3,)),
+            dma((4,)),
+            dma((4,)),
+            dma((8,)),
+            dma((2, 3)),
         ],
-        compiler_params=pltpu.CompilerParams(collective_id=0, has_side_effects=True),
-    )(*blocks, cq.reshape(POS, WIDTH), cg.reshape(POS, WIDTH), xk, xv, length)
+        compiler_params=pltpu.CompilerParams(
+            collective_id=0, has_side_effects=True, vmem_limit_bytes=32 * 2**20
+        ),
+    )(*(pltpu.with_memory_space_constraint(a, pltpu.HBM) for a in arrays), length)
+    count = len(shapes)
+    oq, ok, ov, ocq, otext = pl.pallas_call(
+        lambda *refs: move(count, *refs),
+        name="move",
+        out_shape=shapes,
+        in_specs=[anywhere] * count,
+        out_specs=[anywhere] * count,
+        scratch_shapes=[dma((count,))],
+        compiler_params=pltpu.CompilerParams(vmem_limit_bytes=2**20),
+    )(*grads)
     whole = (1, POS, WIDTH)
-    return oq.reshape(whole), ok.reshape(whole), ov.reshape(whole), ocq.reshape(whole), otext[:, : HEAD_DIM // NX]
+    return oq.reshape(whole), ok.reshape(whole), ov.reshape(whole), ocq.reshape(whole), otext.T
 
 
 def solution(mesh):

time: 123 us -> 112 us (0.911)
  local copies, waits for them, and re-layouts: 6.17 us -> 0 us
  Pallas kernels: 114 us -> 110 us
    unnamed x11 -> x0, local copies, waits for them, and re-layouts: 6.17 us -> none
    pallas_call x1 -> x2, Pallas kernels: 114 us -> 110 us  [the longest x1 109 us: local(): pl.pallas_call(kernel, name='attend_back', out_shape=shapes, in_specs=[pl...]
where the time goes in v2:
time: 112 us; the launch traced here: 111 us
  Pallas kernels  110 us (98%)
  between operations  1.29 us (1%)
    pallas_call x1, Pallas kernels, local(): pl.pallas_call(kernel, name='attend_back', out_shape=shapes, in_specs=[pl...  109 us

profile of v2, /device:TPU:1, one launch (start us, length us, event | category | flops | bytes accessed | tf_op | source)
XLA Modules:
  0.0 111.4 jit_solution(11230412344971565280)
XLA Ops:
  1.3 109.0 %attend_back.1 = (bf16[16,8,1152]{2,1,0:T(8,128)(2,1)S(1)}, bf16[16,8,1152]{2,1,0:T(8,128)(2,1)S(1)}, bf16[16,8,1152]{2,1,0:T(8,128)(2,1)S(1)}, bf16[128,1152]{1,0:T(8,128)(2,1)S(1)}, f32[18,160]{1,0:T(8,128)S(1)}) custom-call(bf16[16,8,1152]{2,1,0:T(8,128)(2,1)} %bitcast.11, bf16[16,8,1152]{2,1,0:T(8,128)(2,1)} %bitcast.12, bf16[16,8,1152]{2,1,0:T(8,128)(2,1)} %bitcast.13, ...), custom_call_target="tpu_custom_call" | custom-call | tf_op jit(solution)/shard_map/attend_back/pallas_call | solution.py:310
  110.3 1.1 move.1

commit v3 on v2

--- a/solution.py
+++ b/solution.py
@@ -99,8 +99,8 @@
 def kernel(
     tq, tk, tv, tg, cq, cg, xk, xv, length,
     oq, ok, ov, ocq, otext,
-    zbuf, pout, pbuf, gbuf, qbuf, zout, tall, tpart, rs1, rsout, rsmine, rsin, rs2out, rs2, rs3out, rs3, cqb, cgb, xkb, xvb,
-    zs, zr, ps, pr, qs, qr, ws, wr, ts, tr, ls, os,
+    zbuf, pout, pbuf, gbuf, qbuf, zout, tall, tpart, rs1, rsout, rsmine, rsin, rs2out, rs2, rs3out, rs3, cqb, cgb, xkb, xvb, vin,
+    zs, zr, ps, pr, qs, qr, ws, wr, ts, tr, ls, os, known,
 ):
     y, z, x = lax.axis_index("seq_0"), lax.axis_index("seq_1"), lax.axis_index("seq_2")
     me = y * NX + x
@@ -119,16 +119,13 @@
         py, px = plane_peer(k)
         return {"seq_0": py, "seq_2": px}
 
+    def at_z(k):
+        return {"seq_1": z_peer(k % NZ)}
+
     barrier = pltpu.get_barrier_semaphore()
-    for k in range(1, NZ):
-        pl.semaphore_signal(barrier, 1, device_id={"seq_1": z_peer(k)}, device_id_type=MESH)
-    for k in range(1, NPL):
-        pl.semaphore_signal(barrier, 1, device_id=in_plane(k), device_id_type=MESH)
-    loads = [pltpu.make_async_copy(*pair, ls.at[i]) for i, pair in enumerate(((cq, cqb), (cg, cgb), (xk, xkb), (xv, xvb)))]
-    loads += [pltpu.make_async_copy(ins[a].at[z], zbuf.at[a, z], ls.at[4 + a]) for a in range(4)]
-    for copy in loads:
-        copy.start()
-    pl.semaphore_wait(barrier, NZ - 1 + NPL - 1)
+    near = [at_z(k) for k in (1, -1, 2, -2)] + [in_plane(k) for k in (1, 3, 4)]
+    for device in near:
+        pl.semaphore_signal(barrier, 1, device_id=device, device_id_type=MESH)
 
     def send(src, dst, send_sem, recv_sem, device):
         pltpu.make_async_remote_copy(
@@ -138,13 +135,37 @@
     def wait_for(ref, sem):
         pltpu.make_async_copy(ref, ref, sem).wait()
 
-    for c, (low, size) in enumerate(IN_CHUNKS):
-        lanes = pl.ds(low, size)
+    own = [pltpu.make_async_copy(ins[a], vin.at[a], ls.at[a]) for a in range(4)]
+    cross = [pltpu.make_async_copy(*pair, ls.at[4 + i]) for i, pair in enumerate(((cq, cqb), (cg, cgb), (xk, xkb), (xv, xvb)))]
+    for copy in own + cross:
+        copy.start()
+    for copy in own:
+        copy.wait()
+
+    def spread(c, distances):
+        lanes = pl.ds(*IN_CHUNKS[c])
         for a in range(4):
-            for k in DISTANCES:
-                peer = z_peer(k)
-                send(ins[a].at[peer, :, lanes], zbuf.at[a, z, :, lanes], zs.at[c, a], zr.at[c, a], {"seq_1": peer})
-    for copy in loads:
+            for k in distances:
+                peer = z_peer(k % NZ)
+                send(vin.at[a, peer, :, lanes], zbuf.at[a, z, :, lanes], zs.at[c, a], zr.at[c, a], {"seq_1": peer})
+
+    def pass_on(i, devices):
+        for device in devices:
+            pl.semaphore_signal(known.at[i], 1, device_id=device, device_id_type=MESH)
+
+    pl.semaphore_wait(barrier, len(near))
+    pass_on(0, (at_z(2), at_z(-2)))
+    spread(0, (2, -2, 1, -1))
+    pl.semaphore_wait(known.at[0], 2)
+    pass_on(1, (at_z(4), at_z(-4)))
+    pass_on(2, [in_plane(k) for k in (1, 3, 4)])
+    spread(0, (4, -4, 3, -3))
+    pl.semaphore_wait(known.at[1], 2)
+    spread(0, (8, 7, -7, 6, -6, 5, -5))
+    spread(1, DISTANCES)
+    for a in range(4):
+        zbuf[a, z] = vin[a, z]
+    for copy in cross:
         copy.wait()
 
     text_rows = lax.broadcasted_iota(jnp.int32, (TEXT, POS), 0)
@@ -165,6 +186,10 @@
         grads = head_back(*(b[:, low:high] for b in (cqb, xkb, xvb, cgb)), head_mask(h), keep)
         for s, grad in zip(sums, grads, strict=True):
             s.add(h, grad)
+
+    pl.semaphore_wait(known.at[2], 3)
+    pass_on(3, (in_plane(4),))
+    pl.semaphore_wait(known.at[3], 1)
 
     for k in range(1, NPL):
         py, px = plane_peer(k)
@@ -334,6 +359,7 @@
             vmem((POS, WIDTH), BF),
             vmem((TEXT, WIDTH), BF),
             vmem((TEXT, WIDTH), BF),
+            vmem((4, NZ, 8, WIDTH), BF),
             dma((2, 4)),
             dma((2, 4)),
             dma((2, 4)),
@@ -346,6 +372,7 @@
             dma((4,)),
             dma((8,)),
             dma((2, 3)),
+            pltpu.SemaphoreType.REGULAR((4,)),
         ],
         compiler_params=pltpu.CompilerParams(
             collective_id=0, has_side_effects=True, vmem_limit_bytes=32 * 2**20

time: 112 us -> 110 us (0.982)
  the two profiles are of different devices: /device:TPU:1 before, /device:TPU:4 now
where the time goes in v3:
time: 110 us
  Pallas kernels  109 us (99%)
  between operations  1.29 us (1%)
    pallas_call x1, Pallas kernels, local(): pl.pallas_call(kernel, name='attend_back', out_shape=shapes, in_specs=[pl...  108 us

profile of v3, /device:TPU:4, one launch (start us, length us, event | category | flops | bytes accessed | tf_op | source)
XLA Modules:
  0.0 110.3 jit_solution(15291112006363156164)
XLA Ops:
  1.3 107.9 %attend_back.1 = (bf16[16,8,1152]{2,1,0:T(8,128)(2,1)S(1)}, bf16[16,8,1152]{2,1,0:T(8,128)(2,1)S(1)}, bf16[16,8,1152]{2,1,0:T(8,128)(2,1)S(1)}, bf16[128,1152]{1,0:T(8,128)(2,1)S(1)}, f32[18,160]{1,0:T(8,128)S(1)}) custom-call(bf16[16,8,1152]{2,1,0:T(8,128)(2,1)} %bitcast.11, bf16[16,8,1152]{2,1,0:T(8,128)(2,1)} %bitcast.12, bf16[16,8,1152]{2,1,0:T(8,128)(2,1)} %bitcast.13, ...), custom_call_target="tpu_custom_call" | custom-call | tf_op jit(solution)/shard_map/attend_back/pallas_call | solution.py:335
  109.2 1.1 move.1

commit v4 on v3

--- a/solution.py
+++ b/solution.py
@@ -243,6 +243,10 @@
     def deliver(c):
         low, size = OUT_CHUNKS[c]
         lanes = pl.ds(low, size)
+
+        def to(peer, a):
+            send(zout.at[a, peer, :, lanes], outs[a].at[z, :, lanes], ws.at[c, a], wr.at[c, a], {"seq_1": peer})
+
         for a in range(3):
             wait_for(qbuf.at[a, pl.ds(0, NPL - 1), :, lanes], qr.at[c, a])
             for t in range(low, low + size, 128):
@@ -250,10 +254,14 @@
                     tall[t // 128, pl.ds(j, NZ, stride=NPL), :] = qbuf[a, j, :, t : t + 128].astype(F32)
                 for f in range(NZ):
                     zout[a, f, :, t : t + 128] = tall[t // 128, NPL * f : NPL * f + NPL, :].astype(BF)
-            for k in DISTANCES:
-                peer = z_peer(k)
-                send(zout.at[a, peer, :, lanes], outs[a].at[z, :, lanes], ws.at[c, a], wr.at[c, a], {"seq_1": peer})
             pltpu.make_async_copy(zout.at[a, z, :, lanes], outs[a].at[z, :, lanes], os.at[c, a]).start()
+            if c == 0:
+                for k in DISTANCES:
+                    to(z_peer(k), a)
+        if c == 1:
+            for i in range(NZ - 1):
+                for a in range(3):
+                    to(i + jnp.where(i >= z, 1, 0), a)
 
     hand_on(0)
 

time: 110 us -> 106 us (0.964)
  the two profiles are of different devices: /device:TPU:4 before, /device:TPU:128 now
where the time goes in v4:
time: 106 us
  Pallas kernels  104 us (98%)
  between operations  1.29 us (1%)
    pallas_call x1, Pallas kernels, local(): pl.pallas_call(kernel, name='attend_back', out_shape=shapes, in_specs=[pl...  103 us

profile of v4, /device:TPU:128, one launch (start us, length us, event | category | flops | bytes accessed | tf_op | source)
XLA Modules:
  0.0 105.8 jit_solution(11909895588583806739)
XLA Ops:
  1.3 103.4 %attend_back.1 = (bf16[16,8,1152]{2,1,0:T(8,128)(2,1)S(1)}, bf16[16,8,1152]{2,1,0:T(8,128)(2,1)S(1)}, bf16[16,8,1152]{2,1,0:T(8,128)(2,1)S(1)}, bf16[128,1152]{1,0:T(8,128)(2,1)S(1)}, f32[18,160]{1,0:T(8,128)S(1)}) custom-call(bf16[16,8,1152]{2,1,0:T(8,128)(2,1)} %bitcast.11, bf16[16,8,1152]{2,1,0:T(8,128)(2,1)} %bitcast.12, bf16[16,8,1152]{2,1,0:T(8,128)(2,1)} %bitcast.13, ...), custom_call_target="tpu_custom_call" | custom-call | tf_op jit(solution)/shard_map/attend_back/pallas_call | solution.py:343
  104.7 1.1 move.1

commit v5 on v4

--- a/solution.py
+++ b/solution.py
@@ -28,6 +28,7 @@
 HEAD_CHUNKS = ((0, 8), (8, 16))
 OUT_CHUNKS = ((0, 512), (512, 640))
 DISTANCES = (8, 7, 9, 6, 10, 5, 11, 4, 12, 3, 13, 2, 14, 1, 15)
+EARLY = 7
 PAIR_DISTANCES = (4, 3, 5, 2, 6, 1, 7)
 TEXT_ROWS = TEXT // NX
 HALF = 640
@@ -258,9 +259,12 @@
             if c == 0:
                 for k in DISTANCES:
                     to(z_peer(k), a)
+            elif a == 0:
+                for i in range(EARLY):
+                    to(i + jnp.where(i >= z, 1, 0), a)
         if c == 1:
             for i in range(NZ - 1):
-                for a in range(3):
+                for a in range(1 if i < EARLY else 0, 3):
                     to(i + jnp.where(i >= z, 1, 0), a)
 
     hand_on(0)

time: 106 us -> 106 us (level)
  the two profiles are of different devices: /device:TPU:128 before, /device:TPU:64 now
where the time goes in v5:
time: 106 us
  Pallas kernels  105 us (99%)
  between operations  1.29 us (1%)
    pallas_call x1, Pallas kernels, local(): pl.pallas_call(kernel, name='attend_back', out_shape=shapes, in_specs=[pl...  104 us

profile of v5, /device:TPU:64, one launch (start us, length us, event | category | flops | bytes accessed | tf_op | source)
XLA Modules:
  0.0 105.9 jit_solution(12156111988612540418)
XLA Ops:
  1.3 103.6 %attend_back.1 = (bf16[16,8,1152]{2,1,0:T(8,128)(2,1)S(1)}, bf16[16,8,1152]{2,1,0:T(8,128)(2,1)S(1)}, bf16[16,8,1152]{2,1,0:T(8,128)(2,1)S(1)}, bf16[128,1152]{1,0:T(8,128)(2,1)S(1)}, f32[18,160]{1,0:T(8,128)S(1)}) custom-call(bf16[16,8,1152]{2,1,0:T(8,128)(2,1)} %bitcast.11, bf16[16,8,1152]{2,1,0:T(8,128)(2,1)} %bitcast.12, bf16[16,8,1152]{2,1,0:T(8,128)(2,1)} %bitcast.13, ...), custom_call_target="tpu_custom_call" | custom-call | tf_op jit(solution)/shard_map/attend_back/pallas_call | solution.py:347
  104.9 1.1 move.1
